TPU v7x, 32 devices: a whole 2x2x4 slice. The times are simulated.
32 devices in a mesh: row: 4 (over x, core), col: 8 (over z, y).
Axes of the slice: x: 2, y: 2, z: 4, core: 2. Of those that a mesh axis runs over, the one named last changes fastest.
Arguments:
- ancestor_inverse: bfloat16 [24576, 24576], P('row', 'col'), may hold values from -0.0390625 to 0.0390625
- panels: bfloat16 [24576, 3, 512], P(('row', 'col')), may hold values from -1.1953125 to 1.1953125
- diag_inverse: float32 [3, 512, 512], replicated, may hold values from -6 to 6
- tile_mask: int32 [3, 192], replicated, may hold values 0 or 1
Outputs:
- off_diagonal: float32 [24576, 3, 512], P(('row', 'col'))
- diagonal: float32 [3, 512, 512], replicated
All inputs are finite; a program needn't handle non-finite values.
Results may differ from a plain program's by a relative error of at most 0.0003.
Values may be sent and summed in bfloat16 or wider, within the bound.
A program may use at most 192 MiB of HBM per device.

v0:
```python
import jax
import jax.numpy as jnp
from jax import lax
from jax.sharding import PartitionSpec as P


def exchange(partial, axis):
    count = lax.axis_size(axis)
    rows, width = partial.shape
    return lax.psum_scatter(partial, axis, scatter_dimension=0, tiled=True)


def body(ancestor_inverse, panels, diag_inverse, tile_mask):
    row_count = lax.axis_size("row")
    col_count = lax.axis_size("col")
    span = lax.axis_index("row") * col_count + lax.axis_index("col")
    kept_rows = panels.shape[0]
    panel_count = panels.shape[1]
    tile = kept_rows * row_count * col_count // tile_mask.shape[1]
    full_mask = jnp.repeat(tile_mask, tile, axis=1).astype(jnp.bfloat16)
    own_mask = lax.dynamic_slice_in_dim(full_mask, span * kept_rows, kept_rows, 1)
    moves = [
        (index, (index % row_count) * col_count + index // row_count)
        for index in range(row_count * col_count)
    ]
    masked = [panels[:, p, :] * own_mask[p][:, None] for p in range(panel_count)]
    sent = [lax.ppermute(block, ("row", "col"), moves) for block in masked]
    sides = [lax.all_gather(block, "row", axis=0, tiled=True) for block in sent]
    results, parts = [], []
    for p in range(panel_count):
        partial = jnp.dot(ancestor_inverse, sides[p], preferred_element_type=jnp.float32)
        summed = -exchange(partial, "col")
        results.append(summed)
        parts.append(
            lax.dot_general(
                masked[p].astype(jnp.float32),
                summed,
                (((0,), (0,)), ((), ())),
                precision=lax.Precision.HIGHEST,
            )
        )
    off_diagonal = jnp.stack(results, axis=1)
    schur = lax.psum(jnp.stack(parts), ("row", "col"))
    return off_diagonal, diag_inverse - schur


def solution(mesh):
    return jax.shard_map(
        body,
        mesh=mesh,
        in_specs=(P("row", "col"), P(("row", "col"), None, None), P(), P()),
        out_specs=(P(("row", "col"), None, None), P()),
        check_vma=False,
    )
```

profile of v0, /device:TPU:0, one launch (start us, length us, event | category | flops | bytes accessed | tf_op | source)
XLA Modules:
  0.0 952.1 jit_solution(13903537531053839367)
XLA Ops:
  7.2 0.7 convert_element_type.10
  7.9 0.1 broadcast_bitcast_fusion
  8.1 0.1 copy.9
  8.2 0.1 dynamic-slice_reduce_fusion.2
  8.3 2.0 bitcast_multiply_fusion.2
  10.3 1.6 collective-permute-start.2
  12.0 1.6 collective-permute-start
  13.6 1.5 collective-permute-start.1
  15.2 86.4 %all-gather.8.cloned.1.call-done = bf16[3072,512]{1,0:T(8,128)(2,1)} async-done(((bf16[768,512]{1,0:T(8,128)(2,1)}), bf16[3072,512]{1,0:T(8,128)(2,1)}) %all-gather.8.cloned.1.call-update) | async-done | bytes 3145744 | tf_op jit(solution)/shard_map/all_gather | solution.py:28
  101.6 27.8 %convolution_bitcast_fusion = f32[6144,512]{0,1:T(8,128)} fusion(bf16[3072,512]{1,0:T(8,128)(2,1)} %all-gather.8.cloned.1.call-done, bf16[6144,3072]{1,0:T(8,128)(2,1)} %param.4), kind=kOutput, calls=%fused_computation | convolution fusion | flops 19327352832 | bytes 53477376 | tf_op jit(solution)/shard_map/dot_general | solution.py:31
  129.4 0.2 reduce-scatter.4.cloned.1.call-start
  129.7 5.6 all-gather.4.cloned.1.call-done
  135.3 27.7 %convolution_bitcast_fusion.2 = f32[6144,512]{0,1:T(8,128)} fusion(bf16[3072,512]{1,0:T(8,128)(2,1)} %all-gather.4.cloned.1.call-done, bf16[6144,3072]{1,0:T(8,128)(2,1)} %param.4), kind=kOutput, calls=%fused_computation.2 | convolution fusion | flops 19327352832 | bytes 53477376 | tf_op jit(solution)/shard_map/dot_general | solution.py:31
  163.1 0.3 reduce-scatter.6.cloned.1.call-start
  163.3 3.3 all-gather.6.cloned.1.call-done
  166.6 27.7 %convolution_bitcast_fusion.1 = f32[6144,512]{0,1:T(8,128)} fusion(bf16[3072,512]{1,0:T(8,128)(2,1)} %all-gather.6.cloned.1.call-done, bf16[6144,3072]{1,0:T(8,128)(2,1)} %param.4), kind=kOutput, calls=%fused_computation.1 | convolution fusion | flops 19327352832 | bytes 53477376 | tf_op jit(solution)/shard_map/dot_general | solution.py:31
  194.3 0.3 all-reduce.2.cloned.1.call-start
  194.6 182.9 %reduce-scatter.8.cloned.1.call-done = f32[768,512]{0,1:T(8,128)} async-done(((f32[6144,512]{0,1:T(8,128)}), f32[768,512]{0,1:T(8,128)}) %reduce-scatter.8.cloned.1.call-update) | async-done | bytes 1572880 | tf_op jit(solution)/shard_map/reduce_scatter | solution.py:10
  377.5 3.1 fusion.12
  380.7 206.9 %reduce-scatter.4.cloned.1.call-done = f32[768,512]{0,1:T(8,128)} async-done(((f32[6144,512]{0,1:T(8,128)}), f32[768,512]{0,1:T(8,128)}) %reduce-scatter.4.cloned.1.call-update) | async-done | bytes 1572880 | tf_op jit(solution)/shard_map/reduce_scatter | solution.py:10
  587.6 3.4 fusion.6
  590.9 206.7 %reduce-scatter.6.cloned.1.call-done = f32[768,512]{0,1:T(8,128)} async-done(((f32[6144,512]{0,1:T(8,128)}), f32[768,512]{0,1:T(8,128)}) %reduce-scatter.6.cloned.1.call-update) | async-done | bytes 1572880 | tf_op jit(solution)/shard_map/reduce_scatter | solution.py:10
  797.6 3.1 fusion.9
  800.7 2.0 pad_maximum_fusion.1
  802.7 1.4 copy-done
  804.1 0.1 negate_bitcast_fusion
  804.2 0.4 copy-done.2
  804.7 0.9 copy-done.1
  805.8 2.4 pad_maximum_fusion
  808.2 6.2 copy.6
  814.4 126.5 %all-reduce.2.cloned.1.call-done = f32[3,512,512]{2,1,0:T(8,128)} async-done(((f32[3,512,512]{2,1,0:T(8,128)}), f32[3,512,512]{2,1,0:T(8,128)}) %all-reduce.2.cloned.1.call-update) | async-done | bytes 3145744 | tf_op jit(solution)/shard_map/psum | solution.py:43
  941.0 4.3 sub.3
  (23 shorter events, 0.5 us)
Async XLA Ops:
  7.2 94.5 %all-gather.8.cloned.1.call-start = ((), (), s32[]{:S(2)}) async-start(), calls=%async_computation.7 | async-start | bytes 3932160 | tf_op jit(solution)/shard_map/all_gather | solution.py:28
  10.3 119.1 %copy-start.4 = (bf16[768,512]{1,0:T(8,128)(2,1)}, bf16[768,512]{1,0:T(8,128)(2,1)S(1)}, u32[]{:S(2)}) copy-start(bf16[768,512]{1,0:T(8,128)(2,1)S(1)} %get-tuple-element.7) | copy-start | bytes 2359300
  10.3 1.6 collective-permute-start.2
  11.9 123.4 %all-gather.4.cloned.1.call-start = ((), (), s32[]{:S(2)}) async-start(), calls=%async_computation.3 | async-start | bytes 3932160 | tf_op jit(solution)/shard_map/all_gather | solution.py:28
  12.0 1.6 collective-permute-start
  13.6 153.1 %all-gather.6.cloned.1.call-start = ((), (), s32[]{:S(2)}) async-start(), calls=%async_computation.5 | async-start | bytes 3932160 | tf_op jit(solution)/shard_map/all_gather | solution.py:28
  13.6 1.5 collective-permute-start.1
  15.2 362.4 %reduce-scatter.8.cloned.1.call-start = ((), (), s32[]{:S(2)}) async-start(), calls=%async_computation.8 | async-start | bytes 14155776 | tf_op jit(solution)/shard_map/reduce_scatter | solution.py:10
  129.4 458.1 %reduce-scatter.4.cloned.1.call-start = ((), (), s32[]{:S(2)}) async-start(), calls=%async_computation.4 | async-start | bytes 14155776 | tf_op jit(solution)/shard_map/reduce_scatter | solution.py:10
  163.1 634.6 %reduce-scatter.6.cloned.1.call-start = ((), (), s32[]{:S(2)}) async-start(), calls=%async_computation.6 | async-start | bytes 14155776 | tf_op jit(solution)/shard_map/reduce_scatter | solution.py:10
  194.3 746.7 %all-reduce.2.cloned.1.call-start = ((), (), s32[]{:S(2)}) async-start(), calls=%async_computation.9 | async-start | bytes 6291456 | tf_op jit(solution)/shard_map/psum | solution.py:43
  802.7 1.4 copy-start
  802.7 1.9 copy-start.2
  804.1 1.5 copy-start.1
  808.2 132.8 %copy-start.3 = (f32[3,512,512]{2,1,0:T(8,128)S(1)}, f32[3,512,512]{2,1,0:T(8,128)}, u32[]{:S(2)}) copy-start(f32[3,512,512]{2,1,0:T(8,128)} %param.6) | copy-start | bytes 9437188
Sparse Core Ops, SparseCore 0:
  12.0 89.5 all-gather.7
  103.2 32.0 all-gather.3
  136.9 29.7 all-gather.5
  170.0 207.4 reduce-scatter.7
  381.0 206.5 reduce-scatter.3
  591.0 206.5 reduce-scatter.5
  803.7 137.2 all-reduce.1
where the time goes:
time: 953 us; the launch traced here: 952 us
  waiting for transfers between devices  818 us (86%)
  matrix products  92.8 us (10%)
  between operations  14.2 us (1%)
  other arithmetic  11.7 us (1%)
    reduce_scatter x3, waiting for transfers between devices, exchange(): return lax.psum_scatter(partial, axis, scatter_dimension=0, tiled=True)  597 us
    psum x1, waiting for transfers between devices, body(): schur = lax.psum(jnp.stack(parts), ('row', 'col'))  127 us
    all_gather x3, waiting for transfers between devices, body(): sides = [lax.all_gather(block, 'row', axis=0, tiled=True) for block in sent]  95.3 us
    dot_general x3, matrix products, body(): jnp.dot(ancestor_inverse, sides[p], preferred_element_type=jnp.float32)  83.2 us
  transfers between devices with their start and end apart: 10, of which 7 were waited for; matrix products, arithmetic and copies ran while one was open for 10% of the time, Pallas kernels for 0%

commit v1 on v0

v1 whole, which is shorter than its diff:
```python
import functools

import jax
import jax.numpy as jnp
from jax import lax
from jax.experimental import pallas as pl
from jax.experimental.pallas import tpu as pltpu
from jax.sharding import PartitionSpec as P

MESH = pl.DeviceIdType.MESH
PAD = 16
STEPS = 64.0
TOP = 32000.0


def line_shape(col_count):
    nz = 4 if col_count % 4 == 0 else 1
    return nz, col_count // nz


def peak(value):
    return jnp.max(jnp.abs(value), axis=0, keepdims=True)


def exponent_of(top):
    return jnp.ceil(jnp.log2(jnp.maximum(top, 1e-33)) * STEPS)


def write_codes(ref, start, value, exponent):
    scale = jnp.exp2(exponent * (-1.0 / STEPS)) * TOP
    codes = jnp.round(value * scale).astype(jnp.int32)
    ref[pl.ds(start, value.shape[0]), :] = codes.astype(jnp.int16)


def write_exponent(ref, start, exponent):
    wide = jnp.broadcast_to(exponent, (PAD, exponent.shape[1]))
    ref[pl.ds(start, PAD), :] = wide.astype(jnp.int32).astype(jnp.int16)


def read_scale(ref, start):
    wide = ref[pl.ds(start, PAD), :].astype(jnp.int32).astype(jnp.float32)
    return jnp.exp2(wide[:1] * (1.0 / STEPS)) * (1.0 / TOP)


def read_codes(ref, start, rows, scale):
    return ref[pl.ds(start, rows), :].astype(jnp.int32).astype(jnp.float32) * scale


def kernel(
    dims, a_ref, *refs
):
    nz, ny, rows, parts, panels, slots = dims
    x_refs, refs = refs[:panels], refs[panels:]
    (
    o_ref, xbuf, abuf, qbuf, pbuf, ysend, yrecv, usend, urecv, dsend, drecv, obuf,
    xsem, asem, yssem, yrsem, ussem, ursem, dssem, drsem, osem,
    ) = refs
    count = panels * parts
    r = lax.axis_index("row")
    c = lax.axis_index("col")
    z = c // ny
    y = lax.rem(c, ny)

    def at(zz, yy):
        return (r, zz * ny + yy)

    def a_copy(t, j):
        s = lax.rem(t, parts)
        slot = lax.rem(t * ny + j, 2)
        yy = lax.rem(y + 1 + j, ny)
        return pltpu.make_async_copy(
            a_ref.at[:, yy, pl.ds(pl.multiple_of(s * rows, rows), rows), :], abuf.at[slot], asem.at[slot]
        )

    def x_copy(p):
        return pltpu.make_async_copy(x_refs[p], xbuf.at[p], xsem.at[p])

    def y_copy(t, j):
        yy = lax.rem(y + 1 + j, ny)
        return pltpu.make_async_remote_copy(
            ysend.at[lax.rem(t, 2), j], yrecv.at[t, j], yssem.at[lax.rem(t, 2), j], yrsem.at[t, j],
            device_id=at(z, yy), device_id_type=MESH,
        )

    def line_copy(t, k, send, recv, ssem, rsem, to):
        size = k * rows + PAD
        slot = lax.rem(t, 2)
        return pltpu.make_async_remote_copy(
            send.at[slot, pl.ds(0, size)], recv.at[t, pl.ds(0, size)], ssem.at[slot], rsem.at[t],
            device_id=at(to, y), device_id_type=MESH,
        )

    def up_copy(t, zz):
        return line_copy(t, nz - 1 - zz, usend, urecv, ussem, ursem, lax.rem(z + 1, nz))

    def down_copy(t, zz):
        return line_copy(t, zz, dsend, drecv, dssem, drsem, lax.rem(z + nz - 1, nz))

    def o_copy(t):
        slot = lax.rem(t, 2)
        p = t // parts
        s = lax.rem(t, parts)
        return pltpu.make_async_copy(
            obuf.at[slot], o_ref.at[p, pl.ds(pl.multiple_of(s * rows, rows), rows), :], osem.at[slot]
        )

    for p in range(panels):
        x_copy(p).start()
    a_copy(0, 0).start()
    a_copy(1 // ny, 1 % ny).start()

    barrier = pltpu.get_barrier_semaphore()
    for j in range(ny - 1):
        pl.semaphore_signal(barrier, inc=1, device_id=at(z, lax.rem(y + 1 + j, ny)), device_id_type=MESH)

    @pl.when(z > 0)
    def _():
        pl.semaphore_signal(barrier, inc=1, device_id=at(lax.rem(z + nz - 1, nz), y), device_id_type=MESH)

    @pl.when(z < nz - 1)
    def _():
        pl.semaphore_signal(barrier, inc=1, device_id=at(lax.rem(z + 1, nz), y), device_id_type=MESH)

    pl.semaphore_wait(
        barrier, ny - 1 + jnp.where(z > 0, 1, 0).astype(jnp.int32) + jnp.where(z < nz - 1, 1, 0).astype(jnp.int32)
    )

    def multiply(t, j, out):
        slot = lax.rem(t * ny + j, 2)
        a_copy(t, j).wait()
        p = t // parts
        for i in range(nz):
            out[pl.ds(i * rows, rows), :] = jnp.dot(abuf[slot, i], xbuf[p], preferred_element_type=jnp.float32)

        @pl.when(t * ny + j + 2 < count * ny)
        def _():
            ahead = j + 2
            a_copy(t + ahead // ny, ahead % ny).start()

    def produce(t):
        for p in range(panels):

            @pl.when(t == p * parts)
            def _():
                x_copy(p).wait()

        slot = lax.rem(t, 2)
        for j in range(ny - 1):
            multiply(t, j, pbuf)

            @pl.when(t >= 2)
            def _():
                y_copy(t - 2, j).wait_send()

            exponent = exponent_of(peak(pbuf[...]))
            for i in range(nz):
                write_codes(ysend.at[slot, j], i * rows, pbuf[pl.ds(i * rows, rows), :], exponent)
            write_exponent(ysend.at[slot, j], nz * rows, exponent)
            y_copy(t, j).start()
        multiply(t, ny - 1, qbuf.at[lax.rem(t, slots)])

    def gather(t):
        q = qbuf.at[lax.rem(t, slots)]
        for j in range(ny - 1):
            y_copy(t, j).wait_recv()
            got = yrecv.at[t, j]
            scale = read_scale(got, nz * rows)
            for i in range(nz):
                q[pl.ds(i * rows, rows), :] += read_codes(got, i * rows, rows, scale)

    def pass_on(t, zz, up):
        send, recv, copy = (usend, urecv, up_copy) if up else (dsend, drecv, down_copy)
        toward = 1 if up else -1
        came = nz - zz if up else zz + 1
        first = zz == (0 if up else nz - 1)
        q = qbuf.at[lax.rem(t, slots)]
        if not first:
            copy(t, zz - toward).wait_recv()
        left = came - 1
        if left == 0:
            return

        @pl.when(t >= 2)
        def _():
            copy(t - 2, zz).wait_send()

        top = None
        if not first:
            scale = read_scale(recv.at[t], came * rows)
        for i in range(left):
            block = pl.ds((zz + toward * (i + 1)) * rows, rows)
            value = q[block, :]
            if not first:
                value = value + read_codes(recv.at[t], (i + 1) * rows, rows, scale)
                q[block, :] = value
            top = peak(value) if top is None else jnp.maximum(top, peak(value))
        exponent = exponent_of(top)
        out = send.at[lax.rem(t, 2)]
        for i in range(left):
            block = pl.ds((zz + toward * (i + 1)) * rows, rows)
            write_codes(out, i * rows, q[block, :], exponent)
        write_exponent(out, left * rows, exponent)
        copy(t, zz).start()

    def finish(t, zz):
        q = qbuf.at[lax.rem(t, slots)]

        @pl.when(t >= 2)
        def _():
            o_copy(t - 2).wait()

        value = q[pl.ds(zz * rows, rows), :]
        if zz > 0:
            value = value + read_codes(urecv.at[t], 0, rows, read_scale(urecv.at[t], (nz - zz) * rows))
        if zz < nz - 1:
            value = value + read_codes(drecv.at[t], 0, rows, read_scale(drecv.at[t], (zz + 1) * rows))
        obuf[lax.rem(t, 2)] = -value
        o_copy(t).start()

    def step(t, carry):
        @pl.when(t < count)
        def _():
            produce(t)

        @pl.when((t >= 1) & (t - 1 < count))
        def _():
            gather(t - 1)

        for zz in range(nz):
            for up in (True, False):
                late = t - 1 - (zz if up else nz - 1 - zz)

                @pl.when((z == zz) & (late >= 0) & (late < count))
                def _():
                    pass_on(late, zz, up)

            @pl.when((z == zz) & (t >= nz))
            def _():
                finish(t - nz, zz)

        return carry

    lax.fori_loop(0, count + nz, step, 0)
    for t in (count - 2, count - 1):
        for j in range(ny - 1):
            y_copy(t, j).wait_send()
        for zz in range(nz):

            @pl.when(z == zz)
            def _():
                if zz < nz - 1:
                    up_copy(t, zz).wait_send()
                if zz > 0:
                    down_copy(t, zz).wait_send()

        o_copy(t).wait()


def product(ancestor_inverse, sides, col_count, kept):
    panels = len(sides)
    depth, width = sides[0].shape
    nz, ny = line_shape(col_count)
    rows = max(d for d in range(16, 129, 16) if kept % d == 0)
    parts = kept // rows
    count = panels * parts
    slots = nz + 1
    dims = (nz, ny, rows, parts, panels, slots)
    a = ancestor_inverse.reshape(nz, ny, kept, depth)
    message, line = nz * rows + PAD, (nz - 1) * rows + PAD
    dma = pltpu.SemaphoreType.DMA
    return pl.pallas_call(
        functools.partial(kernel, dims),
        out_shape=jax.ShapeDtypeStruct((panels, kept, width), jnp.float32),
        in_specs=[pl.BlockSpec(memory_space=pl.ANY)] * (1 + panels),
        out_specs=pl.BlockSpec(memory_space=pl.ANY),
        scratch_shapes=[
            pltpu.VMEM((panels, depth, width), jnp.bfloat16),
            pltpu.VMEM((2, nz, rows, depth), jnp.bfloat16),
            pltpu.VMEM((slots, nz * rows, width), jnp.float32),
            pltpu.VMEM((nz * rows, width), jnp.float32),
            pltpu.VMEM((2, ny - 1, message, width), jnp.int16),
            pltpu.VMEM((count, ny - 1, message, width), jnp.int16),
            pltpu.VMEM((2, line, width), jnp.int16),
            pltpu.VMEM((count, line, width), jnp.int16),
            pltpu.VMEM((2, line, width), jnp.int16),
            pltpu.VMEM((count, line, width), jnp.int16),
            pltpu.VMEM((2, rows, width), jnp.float32),
            dma((panels,)), dma((2,)), dma((2, ny - 1)), dma((count, ny - 1)),
            dma((2,)), dma((count,)), dma((2,)), dma((count,)), dma((2,)),
        ],
        compiler_params=pltpu.CompilerParams(
            collective_id=0, has_side_effects=True, vmem_limit_bytes=66_000_000
        ),
        name="product",
    )(a, *sides)


def body(ancestor_inverse, panels, diag_inverse, tile_mask):
    row_count = lax.axis_size("row")
    col_count = lax.axis_size("col")
    span = lax.axis_index("row") * col_count + lax.axis_index("col")
    kept = panels.shape[0]
    panel_count = panels.shape[1]
    tile = kept * row_count * col_count // tile_mask.shape[1]
    full_mask = jnp.repeat(tile_mask, tile, axis=1).astype(jnp.bfloat16)
    own_mask = lax.dynamic_slice_in_dim(full_mask, span * kept, kept, 1)
    moves = [
        (index, (index % row_count) * col_count + index // row_count)
        for index in range(row_count * col_count)
    ]
    masked = jnp.transpose(panels, (1, 0, 2)) * own_mask[:, :, None]
    sent = [lax.ppermute(masked[p], ("row", "col"), moves) for p in range(panel_count)]
    sides = [lax.all_gather(block, "row", axis=0, tiled=True) for block in sent]
    results = product(ancestor_inverse, sides, col_count, kept)
    high = lax.reduce_precision(results, 8, 7)
    low = (results - high).astype(jnp.bfloat16)
    high = high.astype(jnp.bfloat16)

    def pair(part):
        return lax.dot_general(
            masked, part, (((1,), (1,)), ((0,), (0,))), preferred_element_type=jnp.float32
        )

    schur = lax.psum(pair(high) + pair(low), ("row", "col"))
    return jnp.transpose(results, (1, 0, 2)), diag_inverse - schur


def solution(mesh):
    return jax.shard_map(
        body,
        mesh=mesh,
        in_specs=(P("row", "col"), P(("row", "col"), None, None), P(), P()),
        out_specs=(P(("row", "col"), None, None), P()),
        check_vma=False,
    )
```

time: 953 us -> 572 us (0.60)
  waiting for transfers between devices: 818 us -> 288 us
  Pallas kernels: 0 us -> 243 us
  matrix products: 92.8 us -> 7.73 us
    reduce_scatter x3 -> x0, waiting for transfers between devices: 597 us -> none  [exchange(): return lax.psum_scatter(partial, axis, scatter_dimension=0, tiled=True)]
    pallas_call x0 -> x1, Pallas kernels: none -> 243 us  [product(): pl.pallas_call(functools.partial(kernel, dims), out_shape=jax.ShapeDtypeS...]
    dot_general x6 -> x2, matrix products: 92.8 us -> 7.73 us  [pair(): lax.dot_general(masked, part, (((1,), (1,)), ((0,), (0,))), preferred_ele...]
    all_gather x3, waiting for transfers between devices: 95.3 us -> 153 us  [body(): sides = [lax.all_gather(block, 'row', axis=0, tiled=True) for block in sent]]
  transfers between devices with their start and end apart: 10 -> 7, of which waited for: 7 -> 4; matrix products, arithmetic and copies ran while one was open for 10% -> 0% of each run, Pallas kernels for 0% -> 0%
where the time goes in v1:
time: 572 us
  waiting for transfers between devices  288 us (50%)
  Pallas kernels  243 us (42%)
  between operations  13.9 us (2%)
  local copies, waits for them, and re-layouts  10 us (2%)
  matrix products  7.73 us (1%)
  other arithmetic  7.03 us (1%)
    pallas_call x1, Pallas kernels, product(): pl.pallas_call(functools.partial(kernel, dims), out_shape=jax.ShapeDtypeS...  243 us
    all_gather x3, waiting for transfers between devices, body(): sides = [lax.all_gather(block, 'row', axis=0, tiled=True) for block in sent]  153 us
    psum x1, waiting for transfers between devices, body(): schur = lax.psum(pair(high) + pair(low), ('row', 'col'))  135 us
  transfers between devices with their start and end apart: 7, of which 4 were waited for; matrix products, arithmetic and copies ran while one was open for 0% of the time, Pallas kernels for 0%

profile of v1, /device:TPU:0, one launch (start us, length us, event | category | flops | bytes accessed | tf_op | source)
XLA Modules:
  0.0 571.7 jit_solution(14714350859589162903)
XLA Ops:
  7.2 0.0 all-gather.8.cloned.1.call-start
  7.2 0.7 convert_element_type.13
  7.9 0.1 broadcast_bitcast_fusion
  8.1 0.1 copy.12
  8.2 2.0 bitcast_multiply_fusion
  10.3 0.0 copy-start.1
  10.3 1.4 copy-done.1
  11.7 0.2 slice_bitcast_fusion
  11.8 0.7 collective-permute-start.2
  12.6 0.9 copy-done.4
  13.4 0.0 all-gather.8.cloned.1.call-update
  13.5 0.0 all-gather.6.cloned.1.call-start
  13.5 0.7 collective-permute-start.1
  14.3 0.9 copy-done.5
  15.2 0.0 all-gather.6.cloned.1.call-update
  15.2 0.0 all-gather.4.cloned.1.call-start
  15.2 0.7 collective-permute-start
  16.0 0.0 copy-start.6
  16.0 0.9 copy-done.6
  16.9 0.0 all-gather.4.cloned.1.call-update
  16.9 0.0 all-reduce.2.cloned.1.call-start
  16.9 87.1 %all-gather.8.cloned.1.call-done.refs_2_ = bf16[3072,512]{1,0:T(8,128)(2,1)} async-done(((bf16[768,512]{1,0:T(8,128)(2,1)}), bf16[3072,512]{1,0:T(8,128)(2,1)}) %all-gather.8.cloned.1.call-update) | async-done | bytes 3145744 | tf_op jit(solution)/shard_map/all_gather | solution.py:313
  104.0 33.6 %all-gather.6.cloned.1.call-done.refs_1_ = bf16[3072,512]{1,0:T(8,128)(2,1)} async-done(((bf16[768,512]{1,0:T(8,128)(2,1)}), bf16[3072,512]{1,0:T(8,128)(2,1)}) %all-gather.6.cloned.1.call-update) | async-done | bytes 3145744 | tf_op jit(solution)/shard_map/all_gather | solution.py:313
  137.6 32.8 %all-gather.4.cloned.1.call-done.refs_0_ = bf16[3072,512]{1,0:T(8,128)(2,1)} async-done(((bf16[768,512]{1,0:T(8,128)(2,1)}), bf16[3072,512]{1,0:T(8,128)(2,1)}) %all-gather.4.cloned.1.call-update) | async-done | bytes 3145744 | tf_op jit(solution)/shard_map/all_gather | solution.py:313
  170.4 242.5 %product.1 = f32[3,768,512]{2,1,0:T(8,128)} custom-call(bf16[4,2,768,3072]{3,2,1,0:T(8,128)(2,1)} %bitcast.18, bf16[3072,512]{1,0:T(8,128)(2,1)} %all-gather.4.cloned.1.call-done.refs_0_, bf16[3072,512]{1,0:T(8,128)(2,1)} %all-gather.6.cloned.1.call-done.refs_1_, bf16[3072,512]{1,0:T(8,128)(2,1)} %all-gather.8.cloned.1.call-done.refs_2_), custom_call_target="tpu_custom_call" | custom-call | tf_op jit(solution)/shard_map/product/pallas_call | solution.py:271
  413.0 4.6 fusion.1
  417.6 0.5 copy-done.2
  418.1 3.1 fusion.4
  421.2 0.0 all-reduce.2.cloned.1.call-update
  421.2 134.6 %all-reduce.2.cloned.1.call-done = f32[3,512,512]{2,1,0:T(8,128)} async-done(((f32[3,512,512]{2,1,0:T(8,128)}), f32[3,512,512]{2,1,0:T(8,128)}) %all-reduce.2.cloned.1.call-update) | async-done | bytes 3145744 | tf_op jit(solution)/shard_map/psum | solution.py:324
  555.9 4.3 sub.7
  560.2 5.0 copy.15
  (11 shorter events, 0.0 us)
Async XLA Ops:
  7.2 96.8 %all-gather.8.cloned.1.call-start = ((), (), s32[]{:S(2)}) async-start(), calls=%async_computation.2 | async-start | bytes 3932160 | tf_op jit(solution)/shard_map/all_gather | solution.py:313
  10.3 1.4 copy-start.1
  11.8 0.7 collective-permute-start.2
  12.6 0.9 copy-start.4
  13.5 124.1 %all-gather.6.cloned.1.call-start = ((), (), s32[]{:S(2)}) async-start(), calls=%async_computation.1 | async-start | bytes 3932160 | tf_op jit(solution)/shard_map/all_gather | solution.py:313
  13.5 0.7 collective-permute-start.1
  14.2 0.9 copy-start.5
  15.2 155.2 %all-gather.4.cloned.1.call-start = ((), (), s32[]{:S(2)}) async-start(), calls=%async_computation | async-start | bytes 3932160 | tf_op jit(solution)/shard_map/all_gather | solution.py:313
  15.2 0.7 collective-permute-start
  16.0 0.9 copy-start.6
  16.9 539.0 %all-reduce.2.cloned.1.call-start = ((), (), s32[]{:S(2)}) async-start(), calls=%async_computation.3 | async-start | bytes 6291456 | tf_op jit(solution)/shard_map/psum | solution.py:324
  412.9 4.7 copy-start
  413.0 5.1 copy-start.2
  421.2 134.7 %copy-start.3 = (f32[3,512,512]{2,1,0:T(8,128)S(1)}, f32[3,512,512]{2,1,0:T(8,128)}, u32[]{:S(2)}) copy-start(f32[3,512,512]{2,1,0:T(8,128)} %param.6) | copy-start | bytes 9437188
Sparse Core Ops, SparseCore 0:
  13.6 90.3 all-gather.7
  105.5 32.0 all-gather.5
  139.7 30.6 all-gather.3
  421.3 134.4 all-reduce.1

commit v2 on v1

--- a/solution.py
+++ b/solution.py
@@ -46,13 +46,37 @@
     return ref[pl.ds(start, rows), :].astype(jnp.int32).astype(jnp.float32) * scale
 
 
+class Several:
+    def __init__(self, copies):
+        self.copies = list(copies)
+
+    def start(self):
+        for copy in self.copies:
+            copy.start()
+
+    def wait_send(self):
+        for copy in self.copies:
+            copy.wait_send()
+
+    def wait_recv(self):
+        for copy in self.copies:
+            copy.wait_recv()
+
+
 def kernel(
     dims, a_ref, *refs
 ):
-    nz, ny, rows, parts, panels, slots = dims
-    x_refs, refs = refs[:panels], refs[panels:]
+    nz, ny, nr, rows, parts, panels, slots, whole = dims
+    inputs = 1 if whole else panels
+    x_refs, refs = refs[:inputs], refs[inputs:]
+    if whole:
+        o_ref, s_ref, *refs = refs
+        own, sbuf, gbuf, rc, rx, ry, rz, x1s, x1r, x2s, x2r, x3s, x3r, ownsem, ss, sr, zs, zr, zs2, zr2, outsem = refs[20:]
+        refs = refs[:20]
+    else:
+        o_ref, *refs = refs
     (
-    o_ref, xbuf, abuf, qbuf, pbuf, ysend, yrecv, usend, urecv, dsend, drecv, obuf,
+    xbuf, abuf, qbuf, pbuf, ysend, yrecv, usend, urecv, dsend, drecv, obuf,
     xsem, asem, yssem, yrsem, ussem, ursem, dssem, drsem, osem,
     ) = refs
     count = panels * parts
@@ -75,6 +99,80 @@
     def x_copy(p):
         return pltpu.make_async_copy(x_refs[p], xbuf.at[p], xsem.at[p])
 
+    me = r * (nz * ny) + c
+    goal, place = me // nr, lax.rem(me, nr)
+    across = lax.rem(r + nr // 2, nr)
+    mate = r + 1 - 2 * lax.rem(r, 2)
+
+    def remote(src, dst, ssem, rsem, to):
+        return pltpu.make_async_remote_copy(src, dst, ssem, rsem, device_id=to, device_id_type=MESH)
+
+    def own_copy(p):
+        return pltpu.make_async_copy(x_refs[0].at[p], own.at[p], ownsem.at[p])
+
+    def deal_copy(p, q):
+        size = own.shape[1] // nr
+        return remote(
+            own.at[p, pl.ds(q * size, size)], xbuf.at[p, place, q], x1s.at[p, q], x1r.at[p, place], (q, goal)
+        )
+
+    def deal_wait(p):
+        for k in range(nr):
+
+            @pl.when(c * nr + k != me)
+            def _():
+                spot = xbuf.at[p, k, r]
+                remote(spot, spot, x1s.at[p, 0], x1r.at[p, k], (r, c)).wait_recv()
+
+    def across_copy(p, q):
+        return Several(
+            remote(xbuf.at[p, k, q], xbuf.at[p, k, q], x2s.at[p, k], x2r.at[p, k], (across, c)) for k in range(nr)
+        )
+
+    def mate_copy(p, q, i):
+        return Several(
+            remote(xbuf.at[p, k, q], xbuf.at[p, k, q], x3s.at[p, i, k], x3r.at[p, i, k], (mate, c))
+            for k in range(nr)
+        )
+
+    def deal(p):
+        own_copy(p).wait()
+        size = own.shape[1] // nr
+        for q in range(nr):
+            here = (r == q) & (goal == c)
+
+            @pl.when(jnp.logical_not(here))
+            def _():
+                deal_copy(p, q).start()
+
+            @pl.when(here)
+            def _():
+                xbuf[p, place, q] = own[p, pl.ds(q * size, size), :]
+
+    def share(p):
+        deal_wait(p)
+        across_copy(p, r).start()
+        mate_copy(p, r, 0).start()
+
+    def relay(p):
+        across_copy(p, across).wait_recv()
+        mate_copy(p, across, 1).start()
+
+    def complete(p):
+        mate_copy(p, mate, 0).wait_recv()
+        mate_copy(p, lax.rem(mate + nr // 2, nr), 1).wait_recv()
+
+    def settle(p):
+        for q in range(nr):
+
+            @pl.when(jnp.logical_not((r == q) & (goal == c)))
+            def _():
+                deal_copy(p, q).wait_send()
+
+        across_copy(p, r).wait_send()
+        mate_copy(p, r, 0).wait_send()
+        mate_copy(p, across, 1).wait_send()
+
     def y_copy(t, j):
         yy = lax.rem(y + 1 + j, ny)
         return pltpu.make_async_remote_copy(
@@ -105,7 +203,7 @@
         )
 
     for p in range(panels):
-        x_copy(p).start()
+        (own_copy if whole else x_copy)(p).start()
     a_copy(0, 0).start()
     a_copy(1 // ny, 1 % ny).start()
 
@@ -113,24 +211,34 @@
     for j in range(ny - 1):
         pl.semaphore_signal(barrier, inc=1, device_id=at(z, lax.rem(y + 1 + j, ny)), device_id_type=MESH)
 
-    @pl.when(z > 0)
-    def _():
-        pl.semaphore_signal(barrier, inc=1, device_id=at(lax.rem(z + nz - 1, nz), y), device_id_type=MESH)
-
-    @pl.when(z < nz - 1)
-    def _():
-        pl.semaphore_signal(barrier, inc=1, device_id=at(lax.rem(z + 1, nz), y), device_id_type=MESH)
-
-    pl.semaphore_wait(
-        barrier, ny - 1 + jnp.where(z > 0, 1, 0).astype(jnp.int32) + jnp.where(z < nz - 1, 1, 0).astype(jnp.int32)
-    )
+    for o in range(1, nz):
+        pl.semaphore_signal(barrier, inc=1, device_id=at(lax.rem(z + o, nz), y), device_id_type=MESH)
+    if not whole:
+        pl.semaphore_wait(barrier, ny + nz - 2)
+    else:
+        for to in (across, mate):
+            pl.semaphore_signal(barrier, inc=1, device_id=(to, c), device_id_type=MESH)
+        for k in range(nr):
+            origin = c * nr + k
+
+            @pl.when(origin != me)
+            def _():
+                pl.semaphore_signal(
+                    barrier, inc=1, device_id=(origin // (nz * ny), lax.rem(origin, nz * ny)), device_id_type=MESH
+                )
+
+        pl.semaphore_wait(barrier, ny + nz + nr - jnp.where(goal == c, 1, 0).astype(jnp.int32))
+        deal(0)
+        share(0)
+        relay(0)
 
     def multiply(t, j, out):
         slot = lax.rem(t * ny + j, 2)
         a_copy(t, j).wait()
         p = t // parts
         for i in range(nz):
-            out[pl.ds(i * rows, rows), :] = jnp.dot(abuf[slot, i], xbuf[p], preferred_element_type=jnp.float32)
+            side = xbuf[p].reshape(abuf.shape[-1], xbuf.shape[-1])
+            out[pl.ds(i * rows, rows), :] = jnp.dot(abuf[slot, i], side, preferred_element_type=jnp.float32)
 
         @pl.when(t * ny + j + 2 < count * ny)
         def _():
@@ -142,7 +250,7 @@
 
             @pl.when(t == p * parts)
             def _():
-                x_copy(p).wait()
+                (complete if whole else lambda q: x_copy(q).wait())(p)
 
         slot = lax.rem(t, 2)
         for j in range(ny - 1):
@@ -217,7 +325,123 @@
         obuf[lax.rem(t, 2)] = -value
         o_copy(t).start()
 
+    if whole:
+        half = sbuf.shape[1] // 2
+        low = lax.rem(r, 2)
+        base1 = low * half
+        high = r // 2
+        quarter, eighth, bit = half // 2, half // 4, half // (4 * nz)
+        base2 = base1 + high * quarter
+        base3 = base2 + y * eighth
+        base4 = base3 + z * bit
+
+    def g_at(p, start, size):
+        return gbuf.at[p, pl.ds(pl.multiple_of(start, 8), size)]
+
+    def s_at(p, start, size):
+        return sbuf.at[p, pl.ds(pl.multiple_of(start, 8), size)]
+
+    def swap(p, i):
+        to = ((mate, c), (across, c), at(z, lax.rem(y + 1, ny)))[i % 3]
+        sems = ss.at[p, i], sr.at[p, i]
+        if i < 3:
+            size = (half, quarter, eighth)[i]
+            start = (half * (1 - low), base1 + quarter * (1 - high), base2 + eighth * (1 - y))[i]
+            return remote(s_at(p, start, size), (rc, rx, ry)[i].at[p], *sems, to)
+        size, start = ((half, base1), (quarter, base2), (eighth, base3))[i - 3]
+        return remote(g_at(p, start, size), g_at(p, start, size), *sems, to)
+
+    def swap_wait(p, i):
+        if i < 3:
+            swap(p, i).wait_recv()
+            size, start = ((half, base1), (quarter, base2), (eighth, base3))[i]
+            sbuf[p, pl.ds(pl.multiple_of(start, 8), size), :] += (rc, rx, ry)[i][p]
+        else:
+            size = (half, quarter, eighth)[i - 3]
+            start = (half * (1 - low), base1 + quarter * (1 - high), base2 + eighth * (1 - y))[i - 3]
+            spot = g_at(p, start, size)
+            remote(spot, spot, ss.at[p, i], sr.at[p, i], (r, c)).wait_recv()
+
+    def spread(p, o, back):
+        there = lax.rem(z + o, nz)
+        if back:
+            return remote(g_at(p, base4, bit), g_at(p, base4, bit), zs2.at[p, o - 1], zr2.at[p, o - 1], at(there, y))
+        return remote(
+            s_at(p, base3 + there * bit, bit), rz.at[p, o - 1], zs.at[p, o - 1], zr.at[p, o - 1], at(there, y)
+        )
+
+    def all_sum(p, i):
+        if i == 0:
+            swap(p, 0).start()
+        elif i <= 2:
+            swap_wait(p, i - 1)
+            swap(p, i).start()
+        elif i == 3:
+            swap_wait(p, 2)
+            for o in range(1, nz):
+                spread(p, o, False).start()
+        elif i == 4:
+            for o in range(1, nz):
+                spread(p, o, False).wait_recv()
+            spot = pl.ds(pl.multiple_of(base4, 8), bit)
+            total = sbuf[p, spot, :]
+            for o in range(1, nz):
+                total = total + rz[p, o - 1]
+            gbuf[p, spot, :] = total
+            for o in range(1, nz):
+                spread(p, o, True).start()
+        elif i == 5:
+            for o in range(1, nz):
+                spot = g_at(p, base3 + lax.rem(z - o + nz, nz) * bit, bit)
+                remote(spot, spot, zs2.at[p, 0], zr2.at[p, o - 1], (r, c)).wait_recv()
+            swap(p, 5).start()
+        elif i <= 7:
+            swap_wait(p, 11 - i)
+            swap(p, 10 - i).start()
+        else:
+            swap_wait(p, 3)
+            for k in range(6):
+                swap(p, k).wait_send()
+            for o in range(1, nz):
+                spread(p, o, False).wait_send()
+                spread(p, o, True).wait_send()
+            pltpu.make_async_copy(gbuf.at[p], s_ref.at[p], outsem.at[p]).start()
+
+    def pair(t):
+        p = t // parts
+        s = lax.rem(t, parts)
+
+        @pl.when(s == 0)
+        def _():
+            sbuf[p] = jnp.zeros(sbuf.shape[1:], jnp.float32)
+
+        value = obuf[lax.rem(t, 2)]
+        top = value.astype(jnp.bfloat16)
+        rest = (value - top.astype(jnp.float32)).astype(jnp.bfloat16)
+        mine = own[p, pl.ds(pl.multiple_of(s * rows, rows), rows), :]
+        total = sbuf[p]
+        for part in (top, rest):
+            total = total + lax.dot_general(
+                mine, part, (((0,), (0,)), ((), ())), preferred_element_type=jnp.float32
+            )
+        sbuf[p] = total
+
     def step(t, carry):
+        if whole:
+            for p in range(1, panels):
+
+                @pl.when(t == (p - 1) * parts)
+                def _():
+                    deal(p)
+
+                @pl.when(t == (p - 1) * parts + 2)
+                def _():
+                    share(p)
+
+                @pl.when(t == (p - 1) * parts + 4)
+                def _():
+                    relay(p)
+
         @pl.when(t < count)
         def _():
             produce(t)
@@ -234,13 +458,30 @@
                 def _():
                     pass_on(late, zz, up)
 
-            @pl.when((z == zz) & (t >= nz))
+            @pl.when((z == zz) & (t >= nz) & (t - nz < count))
             def _():
                 finish(t - nz, zz)
 
+        if whole:
+
+            @pl.when((t >= nz) & (t - nz < count))
+            def _():
+                pair(t - nz)
+
+            for i in range(9):
+                since = t - (parts + nz - 1) - i
+
+                @pl.when((since >= 0) & (lax.rem(since + parts * 2, parts) == 0) & (since // parts < panels))
+                def _():
+                    all_sum(since // parts, i)
+
         return carry
 
-    lax.fori_loop(0, count + nz, step, 0)
+    lax.fori_loop(0, count + nz + (8 if whole else 0), step, 0)
+    if whole:
+        for p in range(panels):
+            settle(p)
+            pltpu.make_async_copy(gbuf.at[p], s_ref.at[p], outsem.at[p]).wait()
     for t in (count - 2, count - 1):
         for j in range(ny - 1):
             y_copy(t, j).wait_send()
@@ -256,25 +497,39 @@
         o_copy(t).wait()
 
 
-def product(ancestor_inverse, sides, col_count, kept):
-    panels = len(sides)
-    depth, width = sides[0].shape
+def product(ancestor_inverse, sides, row_count, col_count, kept, panels, whole):
+    depth, width = ancestor_inverse.shape[1], sides[0].shape[-1]
     nz, ny = line_shape(col_count)
     rows = max(d for d in range(16, 129, 16) if kept % d == 0)
     parts = kept // rows
     count = panels * parts
     slots = nz + 1
-    dims = (nz, ny, rows, parts, panels, slots)
+    dims = (nz, ny, row_count, rows, parts, panels, slots, whole)
     a = ancestor_inverse.reshape(nz, ny, kept, depth)
     message, line = nz * rows + PAD, (nz - 1) * rows + PAD
     dma = pltpu.SemaphoreType.DMA
+    side = (panels, depth, width)
+    outs = [jax.ShapeDtypeStruct((panels, kept, width), jnp.float32)]
+    more = []
+    if whole:
+        side = (panels, row_count, row_count, kept // row_count, width)
+        outs.append(jax.ShapeDtypeStruct((panels, width, width), jnp.float32))
+        f32 = lambda *shape: pltpu.VMEM((panels, *shape, width), jnp.float32)
+        more = [
+            pltpu.VMEM((panels, kept, width), jnp.bfloat16),
+            f32(width), f32(width), f32(width // 2), f32(width // 4), f32(width // 8), f32(nz - 1, width // (8 * nz)),
+            dma((panels, row_count)), dma((panels, row_count)), dma((panels, row_count)), dma((panels, row_count)),
+            dma((panels, 2, row_count)), dma((panels, 2, row_count)), dma((panels,)), dma((panels, 6)), dma((panels, 6)),
+            dma((panels, nz - 1)), dma((panels, nz - 1)), dma((panels, nz - 1)), dma((panels, nz - 1)),
+            dma((panels,)),
+        ]
     return pl.pallas_call(
         functools.partial(kernel, dims),
-        out_shape=jax.ShapeDtypeStruct((panels, kept, width), jnp.float32),
-        in_specs=[pl.BlockSpec(memory_space=pl.ANY)] * (1 + panels),
-        out_specs=pl.BlockSpec(memory_space=pl.ANY),
+        out_shape=outs,
+        in_specs=[pl.BlockSpec(memory_space=pl.ANY)] * (1 + len(sides)),
+        out_specs=[pl.BlockSpec(memory_space=pl.ANY)] * len(outs),
         scratch_shapes=[
-            pltpu.VMEM((panels, depth, width), jnp.bfloat16),
+            pltpu.VMEM(side, jnp.bfloat16),
             pltpu.VMEM((2, nz, rows, depth), jnp.bfloat16),
             pltpu.VMEM((slots, nz * rows, width), jnp.float32),
             pltpu.VMEM((nz * rows, width), jnp.float32),
@@ -287,6 +542,7 @@
             pltpu.VMEM((2, rows, width), jnp.float32),
             dma((panels,)), dma((2,)), dma((2, ny - 1)), dma((count, ny - 1)),
             dma((2,)), dma((count,)), dma((2,)), dma((count,)), dma((2,)),
+            *more,
         ],
         compiler_params=pltpu.CompilerParams(
             collective_id=0, has_side_effects=True, vmem_limit_bytes=66_000_000
@@ -309,9 +565,15 @@
         for index in range(row_count * col_count)
     ]
     masked = jnp.transpose(panels, (1, 0, 2)) * own_mask[:, :, None]
+    width = panels.shape[2]
+    nz, ny = line_shape(col_count)
+    whole = row_count == 4 and ny == 2 and nz == 4 and kept % 64 == 0 and kept >= 512 and width % 256 == 0
+    if whole:
+        results, schur = product(ancestor_inverse, [masked], row_count, col_count, kept, panel_count, True)
+        return jnp.transpose(results, (1, 0, 2)), diag_inverse - schur
     sent = [lax.ppermute(masked[p], ("row", "col"), moves) for p in range(panel_count)]
     sides = [lax.all_gather(block, "row", axis=0, tiled=True) for block in sent]
-    results = product(ancestor_inverse, sides, col_count, kept)
+    (results,) = product(ancestor_inverse, sides, row_count, col_count, kept, panel_count, False)
     high = lax.reduce_precision(results, 8, 7)
     low = (results - high).astype(jnp.bfloat16)
     high = high.astype(jnp.bfloat16)

time: 572 us -> 378 us (0.66)
  waiting for transfers between devices: 288 us -> 0 us
  Pallas kernels: 243 us -> 365 us
  between operations: 13.9 us -> 0.69 us
  matrix products: 7.73 us -> 0 us
  local copies, waits for them, and re-layouts: 10 us -> 2.48 us
    all_gather x3 -> x0, waiting for transfers between devices: 153 us -> none  [body(): sides = [lax.all_gather(block, 'row', axis=0, tiled=True) for block in sent]]
    psum x1 -> x0, waiting for transfers between devices: 135 us -> none  [body(): schur = lax.psum(pair(high) + pair(low), ('row', 'col'))]
    pallas_call x1, Pallas kernels: 243 us -> 365 us  [product(): pl.pallas_call(functools.partial(kernel, dims), out_shape=outs, in_specs=...]
    dot_general x2 -> x0, matrix products: 7.73 us -> none  [pair(): lax.dot_general(masked, part, (((1,), (1,)), ((0,), (0,))), preferred_ele...]
    unnamed x17 -> x7, local copies, waits for them, and re-layouts: 9.86 us -> 2.47 us
  transfers between devices with their start and end apart: 7 -> 0, of which waited for: 4 -> 0; matrix products, arithmetic and copies ran while one was open for 0% -> 0% of each run, Pallas kernels for 0% -> 0%
where the time goes in v2:
time: 378 us
  Pallas kernels  365 us (97%)
  other arithmetic  9.58 us (3%)
    pallas_call x1, Pallas kernels, product(): pl.pallas_call(functools.partial(kernel, dims), out_shape=outs, in_specs=...  365 us

profile of v2, /device:TPU:0, one launch (start us, length us, event | category | flops | bytes accessed | tf_op | source)
XLA Modules:
  0.0 377.6 jit_solution(11738474961758625237)
XLA Ops:
  0.6 0.7 convert_element_type.7
  1.3 0.1 broadcast_bitcast_fusion
  1.5 0.1 copy.8
  1.6 3.5 bitcast_multiply_fusion.refs_0_
  5.1 364.9 %product.1 = (f32[3,768,512]{2,1,0:T(8,128)}, f32[3,512,512]{2,1,0:T(8,128)}) custom-call(bf16[4,2,768,3072]{3,2,1,0:T(8,128)(2,1)} %bitcast.9, bf16[3,768,512]{2,1,0:T(8,128)(2,1)} %bitcast_multiply_fusion.refs_0_), custom_call_target="tpu_custom_call" | custom-call | tf_op jit(solution)/shard_map/product/pallas_call | solution.py:526
  370.0 0.0 slice-start
  370.0 0.0 slice-start.1
  370.0 5.4 %sub.3 = f32[3,512,512]{2,1,0:T(8,128)} subtract(f32[3,512,512]{2,1,0:T(8,128)} %param.6, f32[3,512,512]{2,1,0:T(8,128)} %get-tuple-element.5) | non-fusion elementwise | flops 786432 | bytes 9437184 | tf_op jit(solution)/shard_map/sub | solution.py:573
  375.4 0.0 slice-done
  375.4 0.0 slice-done.1
  375.4 2.2 copy.10
  (2 shorter events, 0.0 us)
Async XLA Ops:
  370.0 5.5 %slice-start = ((s8[4718592]{0:T(1024)(128)(4,1)}), s8[4194304]{0:T(1024)(128)(4,1)S(1)}, s32[]{:S(2)}) async-start(s8[4718592]{0:T(1024)(128)(4,1)} %bitcast.10), calls=%async_computation | async-start | bytes 8388608
  370.0 5.4 %slice-start.1 = ((s8[4718592]{0:T(1024)(128)(4,1)}), s8[524288]{0:T(1024)(128)(4,1)S(1)}, s32[]{:S(2)}) async-start(s8[4718592]{0:T(1024)(128)(4,1)} %bitcast.10), calls=%async_computation.1 | async-start | bytes 1048576
